TPU v7x, 32 devices: a whole 2x2x4 slice. The times are simulated.
32 devices in a mesh: gx: 8 (over z, y), gy: 4 (over x, core).
Axes of the slice: x: 2, y: 2, z: 4, core: 2. Of those that a mesh axis runs over, the one named last changes fastest.
Arguments:
- vectors: float32 [64, 32768], P(None, ('gx', 'gy')), may hold values from -6 to 6
- tiles: bfloat16 [4096, 256, 256], P(('gx', 'gy')), may hold values from -0.09375 to 0.09375
- counts: int32 [128], P(('gx', 'gy')), may hold values from 1 to 32, 2112 in all
- tile_col: int32 [4096], P(('gx', 'gy')), may hold values from 0 to 31
- send_list: int32 [32, 32, 1], replicated, may hold values from 0 to 3
Outputs:
- basis: float32 [64, 32768], P(None, ('gx', 'gy'))
- rayleigh: float32 [2, 64, 64], replicated
Inputs may be any that keep to these rules, and one draw needn't show every extreme that they name: The first counts[b] of row block b's 32 slots hold its tiles, the others are ignored.
All inputs are finite; a program needn't handle non-finite values.
Results may differ from a plain program's by a relative error of at most 0.0046.
Values may be sent and summed in bfloat16 or wider, within the bound.
No kernel may reach another device: no remote copies, remote signals or barrier semaphores. Data moves between devices by JAX's collectives and lax.ppermute only.
A program may use at most 64 MiB of HBM per device.

v0:
```python
import jax
import jax.numpy as jnp
from jax import lax
from jax.sharding import PartitionSpec as P

ITERS = 2


def on_device(vectors, tiles, counts, tile_col, send_list):
    me = lax.axis_index(("gx", "gy"))
    devices = lax.axis_size(("gx", "gy"))
    rows_here = vectors.shape[1]
    blocks_here = counts.shape[0]
    tile_size = tiles.shape[1]
    depth = tiles.shape[0] // blocks_here
    width = vectors.shape[0]
    total_rows = rows_here * devices
    live = (jnp.arange(tiles.shape[0], dtype=jnp.int32) % depth < jnp.repeat(counts, depth)).astype(
        jnp.float32
    )
    outgoing = lax.dynamic_index_in_dim(send_list, me, 0, keepdims=False).reshape(-1)
    current = vectors
    rayleigh = []
    for step in range(ITERS):
        rounded = current.astype(jnp.bfloat16)
        own_blocks = rounded.reshape(width, blocks_here, tile_size).transpose(1, 0, 2)
        parcel = jnp.take(own_blocks, outgoing, axis=0)
        arrived = lax.all_to_all(parcel, ("gx", "gy"), split_axis=0, concat_axis=0, tiled=True)
        picked = jnp.take(arrived, tile_col, axis=0)
        prod = jnp.einsum("jrc,jkc->jkr", tiles, picked, preferred_element_type=jnp.float32)
        prod = prod * live[:, None, None]
        image = prod.reshape(blocks_here, depth, width, tile_size).sum(axis=1)
        image = image.transpose(1, 0, 2).reshape(width, rows_here)
        gram_part = jnp.dot(image, image.T, precision=lax.Precision.HIGHEST)
        quotient_part = jnp.dot(current, image.T, precision=lax.Precision.HIGHEST)
        gram, quotient = lax.psum((gram_part, quotient_part), ("gx", "gy"))
        gram = gram / total_rows
        rayleigh.append(quotient / jnp.sqrt(jnp.float32(total_rows)))
        lower = jnp.linalg.cholesky(gram)
        current = lax.linalg.triangular_solve(lower, image, left_side=True, lower=True)
    return (current, jnp.stack(rayleigh))


def solution(mesh):
    return jax.shard_map(
        on_device,
        mesh=mesh,
        in_specs=(
            P(None, ("gx", "gy")),
            P(("gx", "gy"), None, None),
            P(("gx", "gy")),
            P(("gx", "gy")),
            P(),
        ),
        out_specs=(P(None, ("gx", "gy")), P()),
        check_vma=False,
    )
```

profile of v0, /device:TPU:0, one launch (start us, length us, event | category | flops | bytes accessed | tf_op | source)
XLA Modules:
  0.0 203.6 jit_solution(17290401623316212389)
XLA Ops:
  0.6 0.0 copy-start.1
  0.6 0.0 copy-start.2
  0.7 0.7 compare_and_fusion.1
  1.3 1.0 convert_element_type.13
  2.3 0.6 gather_fusion
  2.9 1.2 broadcast_select_fusion
  4.1 7.3 %all-to-all-start = ((bf16[32,64,256]{2,1,0:T(8,128)(2,1)}), bf16[32,64,256]{2,1,0:T(8,128)(2,1)S(1)}, u32[]{:S(2)}, u32[]{:S(2)}) async-start(bf16[32,64,256]{2,1,0:T(8,128)(2,1)} %broadcast_select_fusion), calls=%async_computation | async-start | bytes 2097152 | tf_op jit(solution)/shard_map/all_to_all | solution.py:28
  11.4 0.0 copy-done.1
  11.4 0.1 broadcast_in_dim.24
  11.5 0.1 reshape.67
  11.6 0.0 copy-done.2
  11.6 26.0 %all-to-all-done = bf16[32,64,256]{2,1,0:T(8,128)(2,1)S(1)} async-done(((bf16[32,64,256]{2,1,0:T(8,128)(2,1)}), bf16[32,64,256]{2,1,0:T(8,128)(2,1)S(1)}, u32[]{:S(2)}, u32[]{:S(2)}) %all-to-all-start) | async-done | bytes 1048608 | tf_op jit(solution)/shard_map/all_to_all | solution.py:28
  37.6 2.7 %gather_fusion.1 = bf16[128,64,256]{2,1,0:T(8,128)(2,1)} fusion(bf16[32,64,256]{2,1,0:T(8,128)(2,1)S(1)} %all-to-all-done, s32[1024]{0:T(1024)S(1)} %pad_clamp_fusion), kind=kCustom, calls=%fused_computation.1.clone | custom fusion | bytes 8389120 | tf_op jit(solution)/shard_map/jit(_take)/gather | solution.py:29
  40.4 10.9 %bitcast_reduce_fusion.1 = f32[4,64,256]{2,1,0:T(8,128)S(1)} fusion(f32[128]{0:T(128)S(1)} %get-tuple-element.22, bf16[128,256,256]{2,1,0:T(8,128)(2,1)} %param.13, bf16[128,64,256]{2,1,0:T(8,128)(2,1)} %gather_fusion.1, pred[128]{0:T(512)(128)(4,1)S(1)} %get-tuple-element.21), kind=kOutput, calls=%fused_computation.5 | convolution fusion | flops 1079967744 | bytes 21234304 | tf_op jit(solution)/shard_map/jrc,jkc->jkr/dot_general | solution.py:30
  51.3 0.0 copy-start
  51.3 0.4 convolution_bitcast_fusion.2
  51.6 38.7 %psum.28 = f32[64,64]{0,1:T(8,128)S(1)} all-reduce(f32[64,64]{0,1:T(8,128)S(1)} %convolution_bitcast_fusion.2), channel_id=1, replica_groups=mesh['gx'=8,'gy'=4] {'gx','gy'}, use_global_device_ids=true, to_apply=%region_1.4 | all-reduce | flops 4096 | bytes 32768 | tf_op jit(solution)/shard_map/psum | solution.py:36
  90.3 0.1 copy.38
  90.4 5.8 %cholesky.44 = f32[64,64]{1,0:T(8,128)S(1)} custom-call(f32[64,64]{1,0:T(8,128)S(1)} %fusion.17), custom_call_target="Cholesky" | custom-call | tf_op jit(solution)/shard_map/jit(cholesky)/cholesky | solution.py:39
  96.3 0.6 compare_reduce_fusion.1
  97.0 0.7 fusion.10
  97.6 4.9 %custom-call.6 = f32[1,64,64]{1,2,0:T(8,128)S(1)} custom-call(f32[1,64,64]{2,1,0:T(8,128)S(1)} %fusion.10), custom_call_target="InvertDiagBlocksLowerTriangular" | custom-call | tf_op jit(solution)/shard_map/triangular_solve/custom-call.0 | solution.py:40
  102.6 0.4 fusion.22
  103.0 0.6 gather_fusion.2
  103.6 1.2 broadcast_select_fusion.1
  104.8 4.4 %all-to-all-start.1 = ((bf16[32,64,256]{2,1,0:T(8,128)(2,1)}), bf16[32,64,256]{2,1,0:T(8,128)(2,1)S(1)}, u32[]{:S(2)}, u32[]{:S(2)}) async-start(bf16[32,64,256]{2,1,0:T(8,128)(2,1)} %broadcast_select_fusion.1), calls=%async_computation.1 | async-start | bytes 2097152 | tf_op jit(solution)/shard_map/all_to_all | solution.py:28
  109.1 0.0 copy-done
  109.1 0.4 convolution_bitcast_fusion
  109.5 25.8 %all-to-all-done.1 = bf16[32,64,256]{2,1,0:T(8,128)(2,1)S(1)} async-done(((bf16[32,64,256]{2,1,0:T(8,128)(2,1)}), bf16[32,64,256]{2,1,0:T(8,128)(2,1)S(1)}, u32[]{:S(2)}, u32[]{:S(2)}) %all-to-all-start.1) | async-done | bytes 1048608 | tf_op jit(solution)/shard_map/all_to_all | solution.py:28
  135.3 2.7 %gather_fusion.3 = bf16[128,64,256]{2,1,0:T(8,128)(2,1)} fusion(bf16[32,64,256]{2,1,0:T(8,128)(2,1)S(1)} %all-to-all-done.1, s32[1024]{0:T(1024)S(1)} %pad_clamp_fusion), kind=kCustom, calls=%fused_computation.3.clone | custom fusion | bytes 8389120 | tf_op jit(solution)/shard_map/jit(_take)/gather | solution.py:29
  138.1 10.9 %bitcast_reduce_fusion = f32[4,64,256]{2,1,0:T(8,128)S(1)} fusion(f32[128]{0:T(128)S(1)} %get-tuple-element.22, bf16[128,256,256]{2,1,0:T(8,128)(2,1)} %param.13, bf16[128,64,256]{2,1,0:T(8,128)(2,1)} %gather_fusion.3, pred[128]{0:T(512)(128)(4,1)S(1)} %get-tuple-element.21), kind=kOutput, calls=%fused_computation.4 | convolution fusion | flops 1079967744 | bytes 21234304 | tf_op jit(solution)/shard_map/jrc,jkc->jkr/dot_general | solution.py:30
  149.0 0.4 convolution_bitcast_fusion.1
  149.4 0.4 fusion.23
  149.7 39.8 %all-reduce = (f32[64,64]{0,1:T(8,128)S(1)}, f32[64,64]{0,1:T(8,128)S(1)}, f32[64,64]{0,1:T(8,128)S(1)}) all-reduce(f32[64,64]{0,1:T(8,128)S(1)} %convolution_bitcast_fusion.1, f32[64,64]{0,1:T(8,128)S(1)} %fusion.23, f32[64,64]{0,1:T(8,128)S(1)} %convolution_bitcast_fusion), channel_id=1, replica_groups=mesh['gx'=8,'gy'=4] {'gx','gy'}, use_global_device_ids=true, to_apply=%region_5.10 | all-reduce | flops 12288 | bytes 98304 | tf_op jit(solution)/shard_map/psum | solution.py:36
  189.6 0.7 copy.45
  190.3 0.1 copy.42
  190.4 5.8 %cholesky.55 = f32[64,64]{1,0:T(8,128)S(1)} custom-call(f32[64,64]{1,0:T(8,128)S(1)} %fusion.14), custom_call_target="Cholesky" | custom-call | tf_op jit(solution)/shard_map/jit(cholesky)/cholesky | solution.py:39
  196.3 0.6 compare_reduce_fusion
  196.9 0.7 fusion.11
  197.6 4.9 %custom-call.7 = f32[1,64,64]{1,2,0:T(8,128)S(1)} custom-call(f32[1,64,64]{2,1,0:T(8,128)S(1)} %fusion.11), custom_call_target="InvertDiagBlocksLowerTriangular" | custom-call | tf_op jit(solution)/shard_map/triangular_solve/custom-call.0 | solution.py:40
  202.5 1.1 fusion.12
  (17 shorter events, 0.2 us)
Async XLA Ops:
  0.6 10.8 %copy-start.1 = (s32[4]{0:T(128)S(1)}, s32[4]{0:T(128)}, u32[]{:S(2)}) copy-start(s32[4]{0:T(128)} %param.14) | copy-start | bytes 52
  0.6 11.0 %copy-start.2 = (s32[128]{0:T(128)S(1)}, s32[128]{0:T(128)}, u32[]{:S(2)}) copy-start(s32[128]{0:T(128)} %param.15) | copy-start | bytes 1540
  4.1 33.5 %all-to-all-start = ((bf16[32,64,256]{2,1,0:T(8,128)(2,1)}), bf16[32,64,256]{2,1,0:T(8,128)(2,1)S(1)}, u32[]{:S(2)}, u32[]{:S(2)}) async-start(bf16[32,64,256]{2,1,0:T(8,128)(2,1)} %broadcast_select_fusion), calls=%async_computation | async-start | bytes 2097152 | tf_op jit(solution)/shard_map/all_to_all | solution.py:28
  51.3 57.9 %copy-start = (f32[64,1024]{1,0:T(8,128)S(1)}, f32[64,1024]{1,0:T(8,128)}, u32[]{:S(2)}) copy-start(f32[64,1024]{1,0:T(8,128)} %param.12) | copy-start | bytes 786436
  104.8 30.6 %all-to-all-start.1 = ((bf16[32,64,256]{2,1,0:T(8,128)(2,1)}), bf16[32,64,256]{2,1,0:T(8,128)(2,1)S(1)}, u32[]{:S(2)}, u32[]{:S(2)}) async-start(bf16[32,64,256]{2,1,0:T(8,128)(2,1)} %broadcast_select_fusion.1), calls=%async_computation.1 | async-start | bytes 2097152 | tf_op jit(solution)/shard_map/all_to_all | solution.py:28
where the time goes:
time: 204 us
  blocking collectives  78.5 us (38%)
  waiting for transfers between devices  51.8 us (25%)
  other arithmetic  28.2 us (14%)
  matrix products  24.8 us (12%)
  starting transfers between devices  11.7 us (6%)
  local copies, waits for them, and re-layouts  7.81 us (4%)
    psum x2, blocking collectives, on_device(): gram, quotient = lax.psum((gram_part, quotient_part), ('gx', 'gy'))  78.5 us
    all_to_all x2, waiting for transfers between devices, on_device(): lax.all_to_all(parcel, ('gx', 'gy'), split_axis=0, concat_axis=0, tiled=T...  51.8 us
    dot_general x2, matrix products, on_device(): jnp.einsum('jrc,jkc->jkr', tiles, picked, preferred_element_type=jnp.floa...  21.8 us
    another operation x6, other arithmetic, on_device(): lower = jnp.linalg.cholesky(gram)  13 us
    all_to_all x2, starting transfers between devices, on_device(): lax.all_to_all(parcel, ('gx', 'gy'), split_axis=0, concat_axis=0, tiled=T...  11.7 us
    another operation x4, other arithmetic, on_device(): lax.linalg.triangular_solve(lower, image, left_side=True, lower=True)  11.1 us
    gather x2, local copies, waits for them, and re-layouts, on_device(): picked = jnp.take(arrived, tile_col, axis=0)  5.48 us
  transfers between devices with their start and end apart: 2, of which 2 were waited for; matrix products, arithmetic and copies ran while one was open for 0% of the time, Pallas kernels for 0%

commit v1 on v0

--- a/solution.py
+++ b/solution.py
@@ -33,7 +33,8 @@
         image = image.transpose(1, 0, 2).reshape(width, rows_here)
         gram_part = jnp.dot(image, image.T, precision=lax.Precision.HIGHEST)
         quotient_part = jnp.dot(current, image.T, precision=lax.Precision.HIGHEST)
-        gram, quotient = lax.psum((gram_part, quotient_part), ("gx", "gy"))
+        launch_digits = lambda u_in: lax.psum(lax.psum(u_in, axis_name="gy"), axis_name="gx")
+        gram, quotient = launch_digits((gram_part, quotient_part))
         gram = gram / total_rows
         rayleigh.append(quotient / jnp.sqrt(jnp.float32(total_rows)))
         lower = jnp.linalg.cholesky(gram)

time: 204 us -> 219 us (1.074)
  blocking collectives: 78.5 us -> 95 us
    psum x2 -> x4, blocking collectives: 78.5 us -> 95 us  [the longest x2 71.2 us: on_device(): lax.psum(lax.psum(u_in, axis_name='gy'), axis_name='gx')]
where the time goes in v1:
time: 219 us; the launch traced here: 218 us
  blocking collectives  95 us (43%)
  waiting for transfers between devices  51.8 us (24%)
  other arithmetic  28.2 us (13%)
  matrix products  24.8 us (11%)
  starting transfers between devices  9.97 us (5%)
  local copies, waits for them, and re-layouts  7.81 us (4%)
    psum x2, blocking collectives, on_device(): lax.psum(lax.psum(u_in, axis_name='gy'), axis_name='gx')  71.2 us
    all_to_all x2, waiting for transfers between devices, on_device(): lax.all_to_all(parcel, ('gx', 'gy'), split_axis=0, concat_axis=0, tiled=T...  51.8 us
    psum x2, blocking collectives, on_device(): lax.psum(u_in, axis_name='gy')  23.9 us
    dot_general x2, matrix products, on_device(): jnp.einsum('jrc,jkc->jkr', tiles, picked, preferred_element_type=jnp.floa...  21.8 us
    another operation x6, other arithmetic, on_device(): lower = jnp.linalg.cholesky(gram)  13 us
    another operation x4, other arithmetic, on_device(): lax.linalg.triangular_solve(lower, image, left_side=True, lower=True)  11.1 us
    all_to_all x2, starting transfers between devices, on_device(): lax.all_to_all(parcel, ('gx', 'gy'), split_axis=0, concat_axis=0, tiled=T...  9.97 us
    gather x2, local copies, waits for them, and re-layouts, on_device(): picked = jnp.take(arrived, tile_col, axis=0)  5.48 us
  transfers between devices with their start and end apart: 2, of which 2 were waited for; matrix products, arithmetic and copies ran while one was open for 0% of the time, Pallas kernels for 0%

profile of v1, /device:TPU:0, one launch (start us, length us, event | category | flops | bytes accessed | tf_op | source)
XLA Modules:
  0.0 218.5 jit_solution(273658512589877633)
XLA Ops:
  0.6 0.0 copy-start.1
  0.6 0.0 copy-start.2
  0.7 0.7 compare_and_fusion.1
  1.3 1.0 convert_element_type.13
  2.3 0.6 gather_fusion
  2.9 1.2 broadcast_select_fusion
  4.1 7.3 %all-to-all-start = ((bf16[32,64,256]{2,1,0:T(8,128)(2,1)}), bf16[32,64,256]{2,1,0:T(8,128)(2,1)S(1)}, u32[]{:S(2)}, u32[]{:S(2)}) async-start(bf16[32,64,256]{2,1,0:T(8,128)(2,1)} %broadcast_select_fusion), calls=%async_computation | async-start | bytes 2097152 | tf_op jit(solution)/shard_map/all_to_all | solution.py:28
  11.4 0.0 copy-done.1
  11.4 0.1 broadcast_in_dim.24
  11.5 0.1 reshape.67
  11.6 0.0 copy-done.2
  11.6 26.0 %all-to-all-done = bf16[32,64,256]{2,1,0:T(8,128)(2,1)S(1)} async-done(((bf16[32,64,256]{2,1,0:T(8,128)(2,1)}), bf16[32,64,256]{2,1,0:T(8,128)(2,1)S(1)}, u32[]{:S(2)}, u32[]{:S(2)}) %all-to-all-start) | async-done | bytes 1048608 | tf_op jit(solution)/shard_map/all_to_all | solution.py:28
  37.6 2.7 %gather_fusion.1 = bf16[128,64,256]{2,1,0:T(8,128)(2,1)} fusion(bf16[32,64,256]{2,1,0:T(8,128)(2,1)S(1)} %all-to-all-done, s32[1024]{0:T(1024)S(1)} %pad_clamp_fusion), kind=kCustom, calls=%fused_computation.1.clone | custom fusion | bytes 8389120 | tf_op jit(solution)/shard_map/jit(_take)/gather | solution.py:29
  40.4 10.9 %bitcast_reduce_fusion.1 = f32[4,64,256]{2,1,0:T(8,128)S(1)} fusion(f32[128]{0:T(128)S(1)} %get-tuple-element.25, bf16[128,256,256]{2,1,0:T(8,128)(2,1)} %param.13, bf16[128,64,256]{2,1,0:T(8,128)(2,1)} %gather_fusion.1, pred[128]{0:T(512)(128)(4,1)S(1)} %get-tuple-element.24), kind=kOutput, calls=%fused_computation.5 | convolution fusion | flops 1079967744 | bytes 21234304 | tf_op jit(solution)/shard_map/jrc,jkc->jkr/dot_general | solution.py:30
  51.3 0.4 convolution_bitcast_fusion.2
  51.6 0.0 copy-start
  51.6 11.5 %psum.56 = f32[64,64]{0,1:T(8,128)S(1)} all-reduce(f32[64,64]{0,1:T(8,128)S(1)} %convolution_bitcast_fusion.2), channel_id=1, replica_groups=mesh['gx'=8,'gy'=4] {'gy'}, use_global_device_ids=true, to_apply=%region_1.4 | all-reduce | flops 4096 | bytes 32768 | tf_op jit(solution)/shard_map/psum | solution.py:36
  63.1 35.2 %psum.57 = f32[64,64]{0,1:T(8,128)S(1)} all-reduce(f32[64,64]{0,1:T(8,128)S(1)} %psum.56), channel_id=1, replica_groups=mesh['gx'=8,'gy'=4] {'gx'}, use_global_device_ids=true, to_apply=%region_2.5 | all-reduce | flops 4096 | bytes 32768 | tf_op jit(solution)/shard_map/psum | solution.py:36
  98.3 0.1 copy.38
  98.4 5.8 %cholesky.44 = f32[64,64]{1,0:T(8,128)S(1)} custom-call(f32[64,64]{1,0:T(8,128)S(1)} %fusion.17), custom_call_target="Cholesky" | custom-call | tf_op jit(solution)/shard_map/jit(cholesky)/cholesky | solution.py:40
  104.3 0.6 compare_reduce_fusion.1
  104.9 0.7 fusion.10
  105.6 4.9 %custom-call.6 = f32[1,64,64]{1,2,0:T(8,128)S(1)} custom-call(f32[1,64,64]{2,1,0:T(8,128)S(1)} %fusion.10), custom_call_target="InvertDiagBlocksLowerTriangular" | custom-call | tf_op jit(solution)/shard_map/triangular_solve/custom-call.0 | solution.py:41
  110.5 0.4 fusion.22
  111.0 0.6 gather_fusion.2
  111.6 1.2 broadcast_select_fusion.1
  112.8 2.6 %all-to-all-start.1 = ((bf16[32,64,256]{2,1,0:T(8,128)(2,1)}), bf16[32,64,256]{2,1,0:T(8,128)(2,1)S(1)}, u32[]{:S(2)}, u32[]{:S(2)}) async-start(bf16[32,64,256]{2,1,0:T(8,128)(2,1)} %broadcast_select_fusion.1), calls=%async_computation.1 | async-start | bytes 2097152 | tf_op jit(solution)/shard_map/all_to_all | solution.py:28
  115.4 0.0 copy-done
  115.4 0.4 convolution_bitcast_fusion
  115.8 25.8 %all-to-all-done.1 = bf16[32,64,256]{2,1,0:T(8,128)(2,1)S(1)} async-done(((bf16[32,64,256]{2,1,0:T(8,128)(2,1)}), bf16[32,64,256]{2,1,0:T(8,128)(2,1)S(1)}, u32[]{:S(2)}, u32[]{:S(2)}) %all-to-all-start.1) | async-done | bytes 1048608 | tf_op jit(solution)/shard_map/all_to_all | solution.py:28
  141.6 2.7 %gather_fusion.3 = bf16[128,64,256]{2,1,0:T(8,128)(2,1)} fusion(bf16[32,64,256]{2,1,0:T(8,128)(2,1)S(1)} %all-to-all-done.1, s32[1024]{0:T(1024)S(1)} %pad_clamp_fusion), kind=kCustom, calls=%fused_computation.3.clone | custom fusion | bytes 8389120 | tf_op jit(solution)/shard_map/jit(_take)/gather | solution.py:29
  144.3 10.9 %bitcast_reduce_fusion = f32[4,64,256]{2,1,0:T(8,128)S(1)} fusion(f32[128]{0:T(128)S(1)} %get-tuple-element.25, bf16[128,256,256]{2,1,0:T(8,128)(2,1)} %param.13, bf16[128,64,256]{2,1,0:T(8,128)(2,1)} %gather_fusion.3, pred[128]{0:T(512)(128)(4,1)S(1)} %get-tuple-element.24), kind=kOutput, calls=%fused_computation.4 | convolution fusion | flops 1079967744 | bytes 21234304 | tf_op jit(solution)/shard_map/jrc,jkc->jkr/dot_general | solution.py:30
  155.2 0.4 convolution_bitcast_fusion.1
  155.6 0.4 fusion.23
  156.0 12.4 %all-reduce.1 = (f32[64,64]{0,1:T(8,128)S(1)}, f32[64,64]{0,1:T(8,128)S(1)}, f32[64,64]{0,1:T(8,128)S(1)}) all-reduce(f32[64,64]{0,1:T(8,128)S(1)} %convolution_bitcast_fusion.1, f32[64,64]{0,1:T(8,128)S(1)} %fusion.23, f32[64,64]{0,1:T(8,128)S(1)} %convolution_bitcast_fusion), channel_id=1, replica_groups=mesh['gx'=8,'gy'=4] {'gy'}, use_global_device_ids=true, to_apply=%region_6.11 | all-reduce | flops 12288 | bytes 98304 | tf_op jit(solution)/shard_map/psum | solution.py:36
  168.4 36.0 %all-reduce = (f32[64,64]{0,1:T(8,128)S(1)}, f32[64,64]{0,1:T(8,128)S(1)}, f32[64,64]{0,1:T(8,128)S(1)}) all-reduce(f32[64,64]{0,1:T(8,128)S(1)} %get-tuple-element.17, f32[64,64]{0,1:T(8,128)S(1)} %get-tuple-element.18, f32[64,64]{0,1:T(8,128)S(1)} %get-tuple-element.19), channel_id=1, replica_groups=mesh['gx'=8,'gy'=4] {'gx'}, use_global_device_ids=true, to_apply=%region_7.12 | all-reduce | flops 12288 | bytes 98304 | tf_op jit(solution)/shard_map/psum | solution.py:36
  204.4 0.7 copy.45
  205.1 0.1 copy.42
  205.2 5.8 %cholesky.55 = f32[64,64]{1,0:T(8,128)S(1)} custom-call(f32[64,64]{1,0:T(8,128)S(1)} %fusion.14), custom_call_target="Cholesky" | custom-call | tf_op jit(solution)/shard_map/jit(cholesky)/cholesky | solution.py:40
  211.1 0.6 compare_reduce_fusion
  211.8 0.7 fusion.11
  212.4 4.9 %custom-call.7 = f32[1,64,64]{1,2,0:T(8,128)S(1)} custom-call(f32[1,64,64]{2,1,0:T(8,128)S(1)} %fusion.11), custom_call_target="InvertDiagBlocksLowerTriangular" | custom-call | tf_op jit(solution)/shard_map/triangular_solve/custom-call.0 | solution.py:41
  217.3 1.1 fusion.12
  (17 shorter events, 0.2 us)
Async XLA Ops:
  0.6 10.8 %copy-start.1 = (s32[4]{0:T(128)S(1)}, s32[4]{0:T(128)}, u32[]{:S(2)}) copy-start(s32[4]{0:T(128)} %param.14) | copy-start | bytes 52
  0.6 11.0 %copy-start.2 = (s32[128]{0:T(128)S(1)}, s32[128]{0:T(128)}, u32[]{:S(2)}) copy-start(s32[128]{0:T(128)} %param.15) | copy-start | bytes 1540
  4.1 33.5 %all-to-all-start = ((bf16[32,64,256]{2,1,0:T(8,128)(2,1)}), bf16[32,64,256]{2,1,0:T(8,128)(2,1)S(1)}, u32[]{:S(2)}, u32[]{:S(2)}) async-start(bf16[32,64,256]{2,1,0:T(8,128)(2,1)} %broadcast_select_fusion), calls=%async_computation | async-start | bytes 2097152 | tf_op jit(solution)/shard_map/all_to_all | solution.py:28
  51.6 63.8 %copy-start = (f32[64,1024]{1,0:T(8,128)S(1)}, f32[64,1024]{1,0:T(8,128)}, u32[]{:S(2)}) copy-start(f32[64,1024]{1,0:T(8,128)} %param.12) | copy-start | bytes 786436
  112.8 28.8 %all-to-all-start.1 = ((bf16[32,64,256]{2,1,0:T(8,128)(2,1)}), bf16[32,64,256]{2,1,0:T(8,128)(2,1)S(1)}, u32[]{:S(2)}, u32[]{:S(2)}) async-start(bf16[32,64,256]{2,1,0:T(8,128)(2,1)} %broadcast_select_fusion.1), calls=%async_computation.1 | async-start | bytes 2097152 | tf_op jit(solution)/shard_map/all_to_all | solution.py:28
